TPU v7x, 32 devices: a whole 2x2x4 slice. The times are simulated.
32 devices in a mesh: tensor: 4 (over y, core), context: 8 (over z, x).
Axes of the slice: x: 2, y: 2, z: 4, core: 2. Of those that a mesh axis runs over, the one named last changes fastest.
Arguments:
- tokens: bfloat16 [2048, 5120], P('context', 'tensor'), may hold values from -6 to 6
- query_weight: bfloat16 [5120, 5120], P('context', 'tensor'), may hold values from -0.078125 to 0.078125
- key_weight: bfloat16 [5120, 5120], P('context', 'tensor'), may hold values from -0.078125 to 0.078125
- value_weight: bfloat16 [5120, 5120], P('context', 'tensor'), may hold values from -0.078125 to 0.078125
- cache_keys: bfloat16 [256, 64, 5120], P('context', None, 'tensor'), may hold values from -160 to 160
- cache_values: bfloat16 [256, 64, 5120], P('context', None, 'tensor'), may hold values from -6 to 6
- selected: int32 [16, 32], P('context'), may hold values from -1 to 255, as said below
- counts: int32 [16], P('context'), may hold values from 24 to 32, as said below
- block_slot: int32 [256], replicated, may hold values from 0 to 255, as said below
Outputs:
- attended: bfloat16 [2048, 5120], P('context', 'tensor')
Inputs may be any that keep to these rules, and one draw needn't show every extreme that they name: `selected`: row c names different block ids in its first counts[c] entries and -1 in the others. Among the valid entries of the 2 query blocks of one context device, at most 16 name blocks stored on one context device (block_slot[b] // 32), and exactly 16 do for some device in every draw. `counts`: some query block has 32 valid entries in every draw. `block_slot`: each row of the cache arrays stores exactly one block id.
All inputs are finite; a program needn't handle non-finite values.
Results may differ from a plain program's by a relative error of at most 0.012.
The roundings to bfloat16 on the way count: a program that leaves them out, or rounds other values in their place, can miss the bound.
Values may be sent and summed in bfloat16 or wider, within the bound.
No kernel may reach another device: no remote copies, remote signals or barrier semaphores. Data moves between devices by JAX's collectives and lax.ppermute only.
A program may use at most 192 MiB of HBM per device.

v0:
```python
import jax
import jax.numpy as jnp
from jax import lax
from jax.sharding import PartitionSpec as P

HDIM = 128


NEGATIVE = -1e30


def from_behind(block, axis, distance):
    devices = range(lax.axis_size(axis))
    route = [(i - distance, i) for i in devices if i - distance in devices]
    return lax.ppermute(block, axis, route)


def attend_block(queries, keys_in, values_in, allowed):
    span_count, row_count, feature_width = queries.shape
    head_count = feature_width // HDIM
    query_heads = queries.reshape(span_count, row_count, head_count, HDIM)
    key_heads = keys_in.reshape(span_count, -1, head_count, HDIM)
    value_heads = values_in.reshape(span_count, -1, head_count, HDIM)
    scores = jnp.einsum(
        "cqhd,ckhd->chqk", query_heads, key_heads, preferred_element_type=jnp.float32
    ) * HDIM ** (-0.5)
    opened = allowed[:, None, :, :]
    masked = jnp.where(opened, scores, NEGATIVE)
    highest = jnp.max(masked, axis=3)
    weights = jnp.where(opened, jnp.exp(masked - highest[..., None]), 0.0)
    totals = jnp.sum(weights, axis=3)
    summed = jnp.einsum(
        "chqk,ckhd->chqd",
        weights.astype(jnp.bfloat16),
        value_heads,
        preferred_element_type=jnp.float32,
    )
    return (highest, totals, summed)


def earlier_count(same_group):
    entries = same_group.shape[0]
    position = jnp.arange(entries)
    before = position[None, :] < position[:, None]
    return jnp.sum(jnp.where(same_group & before, 1, 0), axis=1).astype(jnp.int32)


def fill_table(valid_entries, target, payload, length):
    position = jnp.arange(length)
    hits = valid_entries[:, None] & (target[:, None] == position[None, :])
    return jnp.sum(jnp.where(hits, payload[:, None] + 1, 0), axis=0) - 1


def shards(
    tokens,
    query_weight,
    key_weight,
    value_weight,
    cache_keys,
    cache_values,
    selected,
    counts,
    block_slot,
):
    features_all = lax.all_gather(tokens, "tensor", axis=1, tiled=True)
    token_count = features_all.shape[0]
    feature_width = query_weight.shape[1]
    pieces = (
        lax.all_gather(query_weight, "context", axis=0, tiled=True),
        lax.all_gather(key_weight, "context", axis=0, tiled=True),
        lax.all_gather(value_weight, "context", axis=0, tiled=True),
    )
    projected = tuple(
        (
            jnp.dot(features_all, weight_piece, preferred_element_type=jnp.float32)
            for weight_piece in pieces
        )
    )
    span_count = selected.shape[0]
    select_count = selected.shape[1]
    span_rows = token_count // span_count
    query_spans = projected[0].astype(jnp.bfloat16).reshape(span_count, span_rows, feature_width)
    key_spans = projected[1].astype(jnp.bfloat16).reshape(span_count, span_rows, feature_width)
    value_spans = projected[2].astype(jnp.bfloat16).reshape(span_count, span_rows, feature_width)
    before_keys, before_values = from_behind((key_spans[-1], value_spans[-1]), "context", 1)
    prior_keys = jnp.concatenate([before_keys[None], key_spans[:-1]], 0)
    prior_values = jnp.concatenate([before_values[None], value_spans[:-1]], 0)
    local_keys = jnp.concatenate([prior_keys, key_spans], 1)
    local_values = jnp.concatenate([prior_values, value_spans], 1)
    span_index = lax.axis_index("context") * span_count + jnp.arange(span_count)
    prior_open = jnp.broadcast_to(
        (span_index > 0)[:, None, None], (span_count, span_rows, span_rows)
    )
    row_index = jnp.arange(span_rows)
    causal = jnp.broadcast_to(
        (row_index[None, :] <= row_index[:, None])[None], (span_count, span_rows, span_rows)
    )
    local_open = jnp.concatenate([prior_open, causal], 2)
    devices = lax.axis_size("context")
    capacity = max(2, 2 * span_count * select_count // devices)
    stored = cache_keys.shape[0]
    block_rows = cache_keys.shape[1]
    chosen = selected.reshape(-1)
    live_entries = (jnp.arange(select_count)[None, :] < counts[:, None]).reshape(-1)
    matches = chosen[:, None] == jnp.arange(block_slot.shape[0])[None, :]
    slot_rows = jnp.sum(jnp.where(matches, block_slot[None, :], 0), axis=1)
    owner_device = slot_rows // stored
    local_row = slot_rows % stored
    same_owner = (owner_device[:, None] == owner_device[None, :]) & live_entries[None, :]
    span_of = jnp.arange(span_count * select_count) // select_count
    same_span = same_owner & (span_of[:, None] == span_of[None, :])
    target = (owner_device * span_count + span_of) * capacity + earlier_count(same_span)
    wanted = fill_table(live_entries, target, local_row, devices * span_count * capacity).reshape(
        devices, span_count, capacity
    )
    outgoing = jnp.broadcast_to(query_spans[None], (devices, span_count, span_rows, feature_width))
    requested = lax.all_to_all(wanted, "context", split_axis=0, concat_axis=0, tiled=True)
    asked = lax.all_to_all(outgoing, "context", split_axis=0, concat_axis=0, tiled=True)

    def one_source(paired):
        rows_wanted, query_block = paired
        item_count = rows_wanted.shape[0]
        rows_used = jnp.clip(rows_wanted, 0, stored - 1)
        source_keys = jnp.take(cache_keys, rows_used, axis=0).reshape(
            item_count, capacity * block_rows, feature_width
        )
        source_values = jnp.take(cache_values, rows_used, axis=0).reshape(
            item_count, capacity * block_rows, feature_width
        )
        opened = jnp.repeat(rows_wanted >= 0, block_rows, axis=1)
        opened = jnp.broadcast_to(
            opened[:, None, :], (item_count, query_block.shape[1], capacity * block_rows)
        )
        return attend_block(query_block, source_keys, source_values, opened)

    highest_far, totals_far, summed_far = lax.map(one_source, (requested, asked))
    summed_far, highest_far, totals_far = (
        lax.all_to_all(summed_far, "context", split_axis=0, concat_axis=0, tiled=True),
        lax.all_to_all(highest_far, "context", split_axis=0, concat_axis=0, tiled=True),
        lax.all_to_all(totals_far, "context", split_axis=0, concat_axis=0, tiled=True),
    )
    highest_near, totals_near, summed_near = attend_block(
        query_spans, local_keys, local_values, local_open
    )
    peak_score = jnp.maximum(highest_near, jnp.max(highest_far, axis=0))
    near_factor = jnp.exp(highest_near - peak_score)
    far_factor = jnp.exp(highest_far - peak_score[None])
    totals = totals_near * near_factor + jnp.sum(totals_far * far_factor, axis=0)
    summed = summed_near * near_factor[..., None] + jnp.sum(
        summed_far * far_factor[..., None], axis=0
    )
    result = summed / totals[..., None]
    merged = jnp.transpose(result, (0, 2, 1, 3)).reshape(token_count, feature_width)
    return merged.astype(jnp.bfloat16)


def solution(mesh):
    placed = (
        P("context", "tensor"),
        P("context", "tensor"),
        P("context", "tensor"),
        P("context", "tensor"),
        P("context", None, "tensor"),
        P("context", None, "tensor"),
        P("context", None),
        P("context"),
        P(),
    )
    return jax.shard_map(
        shards, mesh=mesh, in_specs=placed, out_specs=P("context", "tensor"), check_vma=False
    )
```

profile of v0, /device:TPU:17, one launch (start us, length us, event | category | flops | bytes accessed | tf_op | source)
XLA Modules:
  0.0 1296.7 jit_solution(9678035795370668421)
XLA Ops:
  17.8 18.1 %all-gather.5.cloned.1.call-done = bf16[256,5120]{1,0:T(8,128)(2,1)} async-done(((bf16[256,1280]{1,0:T(8,128)(2,1)}), bf16[256,5120]{1,0:T(8,128)(2,1)}) %all-gather.5.cloned.1.call-update) | async-done | bytes 2621456 | tf_op jit(solution)/shard_map/all_gather | solution.py:65
  35.9 182.7 %all-gather.7.cloned.1.call-done = bf16[5120,1280]{1,0:T(8,128)(2,1)} async-done(((bf16[640,1280]{1,0:T(8,128)(2,1)}), bf16[5120,1280]{1,0:T(8,128)(2,1)}) %all-gather.7.cloned.1.call-update) | async-done | bytes 13107216 | tf_op jit(solution)/shard_map/all_gather | solution.py:69
  237.8 230.2 %all-to-all-done.1 = bf16[8,2,128,1280]{2,3,1,0:T(8,128)(2,1)} async-done(((bf16[8,2,128,1280]{2,3,1,0:T(8,128)(2,1)}), bf16[8,2,128,1280]{2,3,1,0:T(8,128)(2,1)}, u32[]{:S(2)}, u32[]{:S(2)}) %all-to-all-start.1) | async-done | bytes 5242912 | tf_op jit(solution)/shard_map/all_to_all | solution.py:118
  467.9 533.2 %while.14 = (s32[]{:T(128)}, f32[8,2,10,128]{3,1,2,0:T(2,128)S(1)}, f32[8,2,10,128]{3,1,2,0:T(2,128)S(1)}, f32[8,2,10,128,128]{4,3,2,1,0:T(8,128)}, s32[8,2,16]{...) while((s32[]{:T(128)}, f32[8,2,10,128]{3,1,2,0:T(2,128)S(1)}, ...), condition=%wide.region_7.9_spmd, body=%wide.region_4.8_spmd.sunk | while | flops 1381495040 | bytes 153335056 | solution.py:136
  489.7 11.3 reshape.262
  511.6 11.4 reshape.263
  523.0 11.7 fusion.81
  579.2 11.4 reshape.263
  590.5 11.5 fusion.81
  624.0 11.3 reshape.262
  645.8 11.3 reshape.263
  657.1 11.6 fusion.81
  712.4 11.3 reshape.263
  723.6 11.5 fusion.81
  778.8 11.3 reshape.263
  790.1 11.5 fusion.81
  845.3 11.3 reshape.263
  856.6 11.5 fusion.81
  911.8 11.3 reshape.263
  923.1 11.5 fusion.81
  978.3 11.3 reshape.263
  989.6 11.5 fusion.81
  1001.1 14.2 %all_to_all.25 = f32[8,2,10,128]{3,1,2,0:T(2,128)} all-to-all(f32[8,2,10,128]{3,1,2,0:T(2,128)S(1)} %get-tuple-element.52), channel_id=1, replica_groups=mesh['tensor'=4,'context'=8] {'context'}, dimensions={0} | all-to-all | bytes 163840 | tf_op jit(solution)/shard_map/all_to_all | solution.py:140
  1064.1 201.1 %collective-permute-done = bf16[128,1280]{1,0:T(8,128)(2,1)} collective-permute-done((bf16[128,1280]{1,0:T(8,128)(2,1)}, bf16[128,1280]{1,0:T(8,128)(2,1)}, u32[]{:S(2)}, u32[]{:S(2)}) %collective-permute-start) | collective-permute-done | bytes 327712 | tf_op jit(solution)/shard_map/ppermute | solution.py:15
  (213 shorter events, 431.3 us)
Async XLA Ops:
  6.5 29.4 %all-gather.5.cloned.1.call-start = ((), (), s32[]{:S(2)}) async-start(), calls=%async_computation.5 | async-start | bytes 3276800 | tf_op jit(solution)/shard_map/all_gather | solution.py:65
  7.3 211.4 %all-gather.7.cloned.1.call-start = ((), (), s32[]{:S(2)}) async-start(), calls=%async_computation.6 | async-start | bytes 14745600 | tf_op jit(solution)/shard_map/all_gather | solution.py:69
  8.0 1022.8 %all-gather.9.cloned.1.call-start = ((), (), s32[]{:S(2)}) async-start(), calls=%async_computation.7 | async-start | bytes 14745600 | tf_op jit(solution)/shard_map/all_gather | solution.py:70
  12.2 215.8 %all-to-all-start = ((s32[8,2,16]{2,1,0:T(2,128)}), s32[8,2,16]{2,1,0:T(2,128)S(1)}, u32[]{:S(2)}, u32[]{:S(2)}) async-start(s32[8,2,16]{2,1,0:T(2,128)} %sub.59), calls=%async_computation | async-start | bytes 16384 | tf_op jit(solution)/shard_map/all_to_all | solution.py:117
  227.7 3.8 copy-start.1
  231.4 236.5 %all-to-all-start.1 = ((bf16[8,2,128,1280]{2,3,1,0:T(8,128)(2,1)}), bf16[8,2,128,1280]{2,3,1,0:T(8,128)(2,1)}, u32[]{:S(2)}, u32[]{:S(2)}) async-start(bf16[8,2,128,1280]{2,3,1,0:T(8,128)(2,1)} %broadcast_in_dim.150), calls=%async_computation.1 | async-start | bytes 10485760 | tf_op jit(solution)/shard_map/all_to_all | solution.py:118
  237.2 806.8 %all-gather.11.cloned.1.call-start = ((), (), s32[]{:S(2)}) async-start(), calls=%async_computation.8 | async-start | bytes 14745600 | tf_op jit(solution)/shard_map/all_gather | solution.py:71
  507.7 3.9 copy-start
  574.6 4.5 copy-start
  641.9 3.9 copy-start
  708.4 3.9 copy-start
  774.9 3.9 copy-start
  841.4 3.9 copy-start
  907.9 3.9 copy-start
  974.4 3.9 copy-start
  1023.6 256.3 %all-to-all-start.3 = ((f32[8,2,10,128,128]{4,3,2,1,0:T(8,128)}), f32[8,2,10,128,128]{4,3,2,1,0:T(8,128)}, u32[]{:S(2)}, u32[]{:S(2)}) async-start(f32[8,2,10,128,128]{4,3,2,1,0:T(8,128)} %get-tuple-element.51), calls=%async_computation.3 | async-start | bytes 20971520 | tf_op jit(solution)/shard_map/all_to_all | solution.py:138
  1040.8 17.1 %copy-start.2 = (bf16[256,1280]{1,0:T(8,128)(2,1)S(1)}, bf16[256,1280]{1,0:T(8,128)(2,1)}, u32[]{:S(2)}) copy-start(bf16[256,1280]{1,0:T(8,128)(2,1)} %copy-done.1) | copy-start | bytes 1966084
  1040.8 224.4 %collective-permute-start = (bf16[128,1280]{1,0:T(8,128)(2,1)}, bf16[128,1280]{1,0:T(8,128)(2,1)}, u32[]{:S(2)}, u32[]{:S(2)}) collective-permute-start(bf16[128,1280]{1,0:T(8,128)(2,1)} %get-tuple-element.83), channel_id=1, source_target_pairs={{0,1},{1,2},{2,3},{3,4},{4,5},{5,6},{6,7},{8,9},{9,10},{10,11},{11... | collective-permute-start | bytes 983048 | tf_op jit(solution)/shard_map/ppermute | solution.py:15
  1054.0 218.2 %collective-permute-start.1 = (bf16[128,1280]{1,0:T(8,128)(2,1)}, bf16[128,1280]{1,0:T(8,128)(2,1)}, u32[]{:S(2)}, u32[]{:S(2)}) collective-permute-start(bf16[128,1280]{1,0:T(8,128)(2,1)} %get-tuple-element.81), channel_id=1, source_target_pairs={{0,1},{1,2},{2,3},{3,4},{4,5},{5,6},{6,7},{8,9},{9,10},{10,11},{11... | collective-permute-start | bytes 983048 | tf_op jit(solution)/shard_map/ppermute | solution.py:15
  1057.9 5.0 copy-start.3
  1273.4 5.1 copy-start.6
  1279.8 6.9 copy-start.8
  1279.8 6.9 copy-start.4
  1279.9 6.9 copy-start.5
  (2 other events, 2.6 us)
Sparse Core Ops, SparseCore 0:
  8.9 26.9 all-gather.4
  38.1 180.4 all-gather.6
  220.8 281.6 all-gather.8
  504.5 182.2 all-gather.10
where the time goes:
time: 1300 us
  waiting for transfers between devices  640 us (49%)
  local copies, waits for them, and re-layouts  311 us (24%)
  matrix products  177 us (14%)
  other arithmetic  107 us (8%)
  starting transfers between devices  25.2 us (2%)
  blocking collectives  22.4 us (2%)
  between operations  13.5 us (1%)
    all_to_all x1, waiting for transfers between devices, shards(): lax.all_to_all(outgoing, 'context', split_axis=0, concat_axis=0, tiled=True)  230 us
    ppermute x2, waiting for transfers between devices, from_behind(): return lax.ppermute(block, axis, route)  206 us
    all_gather x1, waiting for transfers between devices, shards(): lax.all_gather(query_weight, 'context', axis=0, tiled=True)  183 us
    dot_general x9, matrix products, attend_block(): jnp.einsum('chqk,ckhd->chqd', weights.astype(jnp.bfloat16), value_heads,...  94.4 us
    reshape x8, local copies, waits for them, and re-layouts, attend_block(): value_heads = values_in.reshape(span_count, -1, head_count, HDIM)  90.4 us
    reshape x8, local copies, waits for them, and re-layouts, attend_block(): key_heads = keys_in.reshape(span_count, -1, head_count, HDIM)  90.1 us
    select_n x8, other arithmetic, one_source(): jnp.take(cache_values, rows_used, axis=0)  72 us
    dot_general x9, matrix products, attend_block(): jnp.einsum('cqhd,ckhd->chqk', query_heads, key_heads, preferred_element_t...  55.6 us
  transfers between devices with their start and end apart: 9, of which 5 were waited for; matrix products, arithmetic and copies ran while one was open for 44% of the time, Pallas kernels for 0%

commit v1 on v0

v1 whole, which is shorter than its diff:
```python
import functools
import math

import jax
import jax.numpy as jnp
from jax import lax
from jax.experimental import pallas as pl
from jax.experimental.pallas import tpu as pltpu
from jax.sharding import PartitionSpec as P

HDIM = 128
LANES = 128
GROUP = 4
STAT_STEP = 32
NEGATIVE = -1e30
SCORE_SCALE = HDIM ** (-0.5)
LOG2E = math.log2(math.e)
BASE2_SCALE = SCORE_SCALE * LOG2E
VMEM_LIMIT = 56 * 1024 * 1024


def params():
    return pltpu.CompilerParams(vmem_limit_bytes=VMEM_LIMIT)


class Grid:
    def __init__(self, tensor, context):
        x_size = max(1, tensor // 2)
        if context % (2 * x_size):
            x_size = 1
        self.T, self.C, self.X = tensor, context, x_size
        self.Z = context // x_size
        self.ZL = self.Z // 2

    def at(self, z, x):
        return (z % self.Z) * self.X + x % self.X

    def move(self, array, target):
        pairs = [(i, target(i // self.X, i % self.X)) for i in range(self.C)]
        return lax.ppermute(array, "context", pairs)

    def shift_x(self, array, step):
        return self.move(array, lambda z, x: self.at(z, x + step))

    def shift_z(self, array, step):
        return self.move(array, lambda z, x: self.at(z + step, x))

    def shift_zl(self, array, step):
        zl = self.ZL
        return self.move(array, lambda z, x: self.at(z // zl * zl + (z % zl + step) % zl, x))

    def swap_half(self, array):
        return self.shift_z(array, self.ZL)


def spread_tokens(grid, tokens):
    T, C, X, ZL = grid.T, grid.C, grid.X, grid.ZL
    half_t = T // 2
    rows, width = tokens.shape
    pairs = []
    for t in range(T):
        for c in range(C):
            z, x = c // X, c % X
            half, low = z // ZL, z % ZL
            goal_t = half * half_t + t % half_t
            goal_c = ((t // half_t) * ZL + low) * X + x
            pairs.append((t * C + c, goal_t * C + goal_c))
    mine = lax.ppermute(tokens, ("tensor", "context"), pairs)
    t = lax.axis_index("tensor")
    y, core = t // 2, t % 2
    y_size = T // 2
    found = []
    for dy in range(y_size):
        block = mine if dy == 0 else lax.ppermute(
            mine, "tensor", [(i, ((i // 2 + dy) % y_size) * 2 + i % 2) for i in range(T)]
        )
        twin = lax.ppermute(block, "tensor", [(i, i ^ 1) for i in range(T)])
        found.append(((y - dy) % y_size * 2 + core, block))
        found.append(((y - dy) % y_size * 2 + 1 - core, twin))
    whole = jnp.zeros((2, rows, half_t * width), tokens.dtype)
    for source, block in found:
        whole = lax.dynamic_update_slice(
            whole, block[None], (source // half_t, 0, source % half_t * width)
        )
    return whole


def gather_weight(grid, weight):
    rows = weight.shape[0]
    cut = max(LANES, rows // 2 // LANES * LANES)
    top, low = weight[:cut], weight[cut:]
    blocks = {(0, 0): [weight]}
    for dx in range(1, grid.X):
        blocks[(0, dx)] = [grid.shift_x(top, dx), grid.shift_x(low, dx)]
    for dz in range(1, grid.ZL):
        near_low = grid.shift_zl(low, dz)
        near_top = grid.shift_zl(top, dz)
        blocks[(dz, 0)] = [near_top, near_low]
        for dx in range(1, grid.X):
            blocks[(dz, dx)] = [
                grid.shift_zl(blocks[(0, dx)][0], dz),
                grid.shift_x(near_low, dx),
            ]
    return blocks


def project_body(piece_counts, *refs):
    n = len(piece_counts)
    total = None
    at = n
    for index in range(n):
        start = 0
        for _ in range(piece_counts[index]):
            w_ref = refs[at]
            at += 1
            depth = w_ref.shape[0]
            part = jnp.dot(
                refs[index][:, start : start + depth], w_ref[...], preferred_element_type=jnp.float32
            )
            start += depth
            total = part if total is None else total + part
    refs[at][...] = total.astype(refs[at].dtype)


def project(features, pieces, out_type):
    rows = features[0].shape[0]
    columns = pieces[0][0].shape[1]
    tile = 256 if columns % 256 == 0 else LANES
    flat = [w for block in pieces for w in block]
    depth = sum(w.shape[0] for w in flat)
    return pl.pallas_call(
        functools.partial(project_body, tuple(len(block) for block in pieces)),
        grid=(columns // tile,),
        in_specs=[pl.BlockSpec(f.shape, lambda j: (0, 0)) for f in features]
        + [pl.BlockSpec((w.shape[0], tile), lambda j: (0, j)) for w in flat],
        out_specs=pl.BlockSpec((rows, tile), lambda j: (0, j)),
        out_shape=jax.ShapeDtypeStruct((rows, columns), out_type),
        compiler_params=params(),
        cost_estimate=pl.CostEstimate(
            flops=2 * rows * depth * columns,
            bytes_accessed=2 * depth * (columns + rows) + 4 * rows * columns,
            transcendentals=0,
        ),
        name="project",
    )(*features, *flat)


def code_stats(stats):
    high = stats.astype(jnp.bfloat16).astype(jnp.float32)
    rest = stats - high
    middle = rest.astype(jnp.bfloat16).astype(jnp.float32)
    low = (rest - middle).astype(jnp.bfloat16).astype(jnp.float32)
    return (high + pltpu.roll(middle, STAT_STEP, 1) + pltpu.roll(low, 2 * STAT_STEP, 1)).astype(
        jnp.bfloat16
    )


def read_stats(coded):
    coded = coded.astype(jnp.float32)
    return (
        coded
        + pltpu.roll(coded, LANES - STAT_STEP, 1)
        + pltpu.roll(coded, LANES - 2 * STAT_STEP, 1)
    )


def write_partial(out_ref, rows, head_count, peak_of, both_of):
    lane = lax.broadcasted_iota(jnp.int32, (rows.size, LANES), 1)
    stats = jnp.zeros((rows.size, LANES), jnp.float32)
    for h in range(head_count):
        both = both_of(h)
        total = both[:, HDIM:]
        live = total > 0.0
        safe = jnp.where(live, total, 1.0)
        out_ref[rows, h * HDIM : (h + 1) * HDIM] = (both[:, :HDIM] / safe).astype(out_ref.dtype)
        log_sum = jnp.where(live, peak_of(h) * BASE2_SCALE + jnp.log2(safe), NEGATIVE)
        stats = jnp.where(lane == h, log_sum, stats)
    out_ref[rows, head_count * HDIM :] = code_stats(stats)


def far_body(item_count, table_ref, source_ref, q_ref, *refs):
    keys, values = refs[:GROUP], refs[GROUP : 2 * GROUP]
    out_ref, peak_ref, both_ref = refs[2 * GROUP :]
    head_count = q_ref.shape[1] // HDIM
    row_count = q_ref.shape[0]
    block_rows = keys[0].shape[1]
    base = (source_ref[0] * item_count + pl.program_id(0)) * 8
    live = table_ref[base + 1]

    @pl.when(table_ref[base + 2] > 0)
    def _():
        peak_ref[...] = jnp.full(peak_ref.shape, NEGATIVE, jnp.float32)
        both_ref[...] = jnp.zeros(both_ref.shape, jnp.float32)

    @pl.when(live > 0)
    def _():
        lane = lax.broadcasted_iota(jnp.int32, (row_count, GROUP * block_rows), 1)
        open_keys = lane < live * block_rows
        ones = jnp.ones((GROUP * block_rows, HDIM), jnp.bfloat16)
        for h in range(head_count):
            part = slice(h * HDIM, (h + 1) * HDIM)
            key = jnp.concatenate([k[0, :, part] for k in keys], 0)
            value = jnp.concatenate([v[0, :, part] for v in values], 0)
            scores = lax.dot_general(
                q_ref[:, part], key, (((1,), (1,)), ((), ())), preferred_element_type=jnp.float32
            )
            scores = jnp.where(open_keys, scores, NEGATIVE)
            before = peak_ref[h]
            peak = jnp.maximum(before, jnp.max(scores, axis=1, keepdims=True))
            fade = jnp.exp2((before - peak) * BASE2_SCALE)
            weights = jnp.exp2((scores - peak[:, :1]) * BASE2_SCALE).astype(jnp.bfloat16)
            grown = jnp.dot(
                weights, jnp.concatenate([value, ones], 1), preferred_element_type=jnp.float32
            )
            peak_ref[h] = peak
            both_ref[h] = both_ref[h] * jnp.concatenate([fade, fade], 1) + grown

    @pl.when(table_ref[base + 3] > 0)
    def _():
        write_partial(
            out_ref, pl.ds(0, row_count), head_count, lambda h: peak_ref[h], lambda h: both_ref[h]
        )


def far_partial(queries, source, table, item_count, cache_keys, cache_values, span_rows):
    rows, width = queries.shape
    head_count = width // HDIM
    block_rows = cache_keys.shape[1]

    def field(i, tab, src, which):
        return tab[(src[0] * item_count + i) * 8 + which]

    def span_map(i, tab, src):
        return (field(i, tab, src, 0), 0)

    def row_map(g):
        return lambda i, tab, src: (field(i, tab, src, 4 + g), 0, 0)

    block_specs = [pl.BlockSpec((1, block_rows, width), row_map(g)) for g in range(GROUP)]
    return pl.pallas_call(
        functools.partial(far_body, item_count),
        grid_spec=pltpu.PrefetchScalarGridSpec(
            num_scalar_prefetch=2,
            grid=(item_count,),
            in_specs=[pl.BlockSpec((span_rows, width), span_map)] + block_specs + block_specs,
            out_specs=pl.BlockSpec((span_rows, width + LANES), span_map),
            scratch_shapes=[
                pltpu.VMEM((head_count, span_rows, HDIM), jnp.float32),
                pltpu.VMEM((head_count, span_rows, 2 * HDIM), jnp.float32),
            ],
        ),
        out_shape=jax.ShapeDtypeStruct((rows, width + LANES), jnp.bfloat16),
        compiler_params=params(),
        cost_estimate=pl.CostEstimate(
            flops=4 * rows * width * GROUP * block_rows * 8,
            bytes_accessed=2 * GROUP * block_rows * width * 2 * item_count,
            transcendentals=rows * head_count * GROUP * block_rows,
        ),
        name="far",
    )(table, source, queries, *([cache_keys] * GROUP), *([cache_values] * GROUP))


def near_body(first_ref, q_ref, k_ref, v_ref, pk_ref, pv_ref, out_ref):
    rows, width = q_ref.shape
    span_rows = pk_ref.shape[0]
    head_count = width // HDIM
    row = lax.broadcasted_iota(jnp.int32, (span_rows, 2 * span_rows), 0)
    lane = lax.broadcasted_iota(jnp.int32, (span_rows, 2 * span_rows), 1)
    causal = lane - span_rows <= row
    ones = jnp.ones((2 * span_rows, HDIM), jnp.bfloat16)
    for j in range(rows // span_rows):
        here = pl.ds(j * span_rows, span_rows)
        opened = causal if j else causal & (lane >= first_ref[0])
        peaks, boths = [], []
        for h in range(head_count):
            part = slice(h * HDIM, (h + 1) * HDIM)
            if j:
                both_rows = pl.ds((j - 1) * span_rows, 2 * span_rows)
                key, value = k_ref[both_rows, part], v_ref[both_rows, part]
            else:
                key = jnp.concatenate([pk_ref[:, part], k_ref[:span_rows, part]], 0)
                value = jnp.concatenate([pv_ref[:, part], v_ref[:span_rows, part]], 0)
            scores = lax.dot_general(
                q_ref[here, part], key, (((1,), (1,)), ((), ())), preferred_element_type=jnp.float32
            )
            scores = jnp.where(opened, scores, NEGATIVE)
            peak = jnp.max(scores, axis=1, keepdims=True)
            weights = jnp.exp2((scores - peak) * BASE2_SCALE).astype(jnp.bfloat16)
            peaks.append(peak)
            boths.append(
                jnp.dot(weights, jnp.concatenate([value, ones], 1), preferred_element_type=jnp.float32)
            )
        write_partial(
            out_ref, here, head_count,
            lambda h: jnp.broadcast_to(peaks[h], (span_rows, LANES)), lambda h: boths[h],
        )


def near_partial(queries, new_keys, new_values, prior_keys, prior_values, first):
    rows, width = queries.shape
    whole = pl.BlockSpec(memory_space=pltpu.VMEM)
    return pl.pallas_call(
        near_body,
        in_specs=[pl.BlockSpec(memory_space=pltpu.SMEM)] + [whole] * 5,
        out_specs=whole,
        out_shape=jax.ShapeDtypeStruct((rows, width + LANES), jnp.bfloat16),
        compiler_params=params(),
        cost_estimate=pl.CostEstimate(
            flops=4 * rows * width * prior_keys.shape[0] * 8,
            bytes_accessed=10 * rows * width,
            transcendentals=rows * width,
        ),
        name="near",
    )(first, queries, new_keys, new_values, prior_keys, prior_values)


def merge_body(count, coded, *refs):
    out_ref = refs[count]
    width = refs[0].shape[1] - LANES
    stats = [read_stats(refs[i][:, width:]) for i in range(count)]
    peak = functools.reduce(jnp.maximum, stats)
    shares = [jnp.exp2(s - peak) for s in stats]
    total = functools.reduce(jnp.add, shares)
    shares = [s / total for s in shares]
    for h in range(width // HDIM):
        part = slice(h * HDIM, (h + 1) * HDIM)
        summed = None
        for i in range(count):
            term = refs[i][:, part].astype(jnp.float32) * shares[i][:, h : h + 1]
            summed = term if summed is None else summed + term
        out_ref[:, part] = summed.astype(out_ref.dtype)
    if coded:
        lane = lax.broadcasted_iota(jnp.int32, peak.shape, 1)
        log_sum = jnp.where(lane < width // HDIM, peak + jnp.log2(total), 0.0)
        out_ref[:, width:] = code_stats(log_sum)


def merge(partials, coded):
    rows, full = partials[0].shape
    width = full if coded else full - LANES
    tile = rows // 2
    return pl.pallas_call(
        functools.partial(merge_body, len(partials), coded),
        grid=(2,),
        in_specs=[pl.BlockSpec((tile, full), lambda i: (i, 0))] * len(partials),
        out_specs=pl.BlockSpec((tile, width), lambda i: (i, 0)),
        out_shape=jax.ShapeDtypeStruct((rows, width), jnp.bfloat16),
        compiler_params=params(),
        cost_estimate=pl.CostEstimate(
            flops=rows * full * 4 * len(partials) * 64,
            bytes_accessed=2 * rows * full * (len(partials) + 1),
            transcendentals=rows * LANES * len(partials),
        ),
        name="merge",
    )(*partials)


def work_table(selected, counts, block_slot, stored, capacity, place):
    spans, select = selected.shape
    packed = jnp.concatenate([selected, counts[:, None]], 1)
    packed = lax.all_gather(packed, "context", axis=0, tiled=True)
    chosen, live_count = packed[:, :select], packed[:, select:]
    entry = jnp.arange(select)
    match = chosen[:, :, None] == jnp.arange(block_slot.shape[0])[None, None, :]
    slot = jnp.sum(jnp.where(match, block_slot[None, None, :], 0), axis=2)
    mine = (entry[None, :] < live_count) & (slot // stored == place)
    earlier = entry[None, :] < entry[:, None]
    rank = jnp.sum(jnp.where(mine[:, None, :] & earlier[None], 1, 0), axis=2)
    position = jnp.arange(capacity)
    hits = mine[:, :, None] & (rank[:, :, None] == position[None, None, :])
    rows = jnp.sum(jnp.where(hits, (slot % stored)[:, :, None], 0), axis=1)
    rows = rows.reshape(-1, spans, capacity)
    held = jnp.sum(jnp.where(mine, 1, 0), axis=1).reshape(-1, spans)
    groups = jnp.maximum(1, (held + GROUP - 1) // GROUP)
    ends = jnp.cumsum(groups, axis=1)
    item_count = capacity // GROUP + spans - 1
    item = jnp.arange(item_count)[None, :]
    active = item < ends[:, -1:]
    item = jnp.minimum(item, ends[:, -1:] - 1)
    span = jnp.sum(jnp.where(item[:, :, None] >= ends[:, None, :], 1, 0), axis=2)
    own = span[:, :, None] == jnp.arange(spans)[None, None, :]
    pick = lambda a: jnp.sum(jnp.where(own, a[:, None, :], 0), axis=2)
    chunk = item - pick(ends - groups)
    live = jnp.where(active, jnp.clip(pick(held) - chunk * GROUP, 0, GROUP), 0)
    first = jnp.where(active & (chunk == 0), 1, 0)
    last = jnp.where(active & (chunk == pick(groups) - 1), 1, 0)
    fields = [span, live, first, last]
    for g in range(GROUP):
        wanted = (chunk * GROUP + g)[:, :, None, None] == position[None, None, None, :]
        fields.append(
            jnp.sum(jnp.where(own[..., None] & wanted, rows[:, None], 0), axis=(2, 3))
        )
    return jnp.stack(fields, axis=2).astype(jnp.int32).reshape(-1), item_count


def shards(
    tokens, query_weight, key_weight, value_weight, cache_keys, cache_values, selected, counts, block_slot
):
    grid = Grid(lax.axis_size("tensor"), lax.axis_size("context"))
    X, Z, ZL = grid.X, grid.Z, grid.ZL
    place = lax.axis_index("context")
    z, x = place // X, place % X
    half, low = z // ZL, z % ZL
    spans, select = selected.shape
    rows = tokens.shape[0]
    span_rows = rows // spans
    capacity = max(GROUP, 2 * spans * select // grid.C)
    table, item_count = work_table(
        selected, counts, block_slot, cache_keys.shape[0], capacity, place
    )

    query_blocks = gather_weight(grid, query_weight)
    order = list(query_blocks)
    whole = spread_tokens(grid, tokens)
    depth = query_weight.shape[0]

    def features_of(which):
        return [
            lax.dynamic_slice(
                whole,
                (which, 0, ((low - dz) % ZL * X + (x - dx) % X) * depth),
                (1, rows, depth),
            )[0]
            for dz, dx in order
        ]

    other_features, own_features = features_of(1 - half), features_of(half)

    def product(blocks, features, out_type):
        return project(features, [blocks[key] for key in order], out_type)

    sent = product(query_blocks, other_features, jnp.float32)
    arrived = grid.swap_half(sent)
    kept = product(query_blocks, own_features, jnp.float32)
    queries = (kept + arrived).astype(jnp.bfloat16)

    def narrow_project(weight, after):
        weight, _ = lax.optimization_barrier((weight, after))
        blocks = gather_weight(grid, weight)
        there = product(blocks, other_features, jnp.bfloat16)
        here = product(blocks, own_features, jnp.float32)
        back = grid.swap_half(there)
        return (here + back.astype(jnp.float32)).astype(jnp.bfloat16)

    new_keys = narrow_project(key_weight, sent)

    by_z = [queries] + [grid.shift_z(queries, k) for k in range(1, Z)]
    merged = []
    for k in range(Z):
        partials = {}
        for dx in list(range(1, X)) + [0]:
            asked = grid.shift_x(by_z[k], dx) if dx else by_z[k]
            source = grid.at(z - k, x - dx).astype(jnp.int32).reshape(1)
            partials[dx] = far_partial(
                asked, source, table, item_count, cache_keys, cache_values, span_rows
            )
        together = [partials[0]] + [grid.shift_x(partials[dx], -dx) for dx in range(1, X)]
        merged.append(merge(together, True) if X > 1 else together[0])
    returned = [merged[0]] + [grid.shift_z(merged[k], -k) for k in range(1, Z)]

    new_values = narrow_project(value_weight, queries)
    ends = jnp.stack([new_keys[rows - span_rows :], new_values[rows - span_rows :]])
    prior = lax.ppermute(ends, "context", [(i - 1, i) for i in range(1, grid.C)])
    first = jnp.where(place == 0, span_rows, 0).astype(jnp.int32).reshape(1)
    near = near_partial(queries, new_keys, new_values, prior[0], prior[1], first)
    return merge(returned + [near], False)


def solution(mesh):
    placed = (
        P("context", "tensor"),
        P("context", "tensor"),
        P("context", "tensor"),
        P("context", "tensor"),
        P("context", None, "tensor"),
        P("context", None, "tensor"),
        P("context", None),
        P("context"),
        P(),
    )
    return jax.shard_map(
        shards, mesh=mesh, in_specs=placed, out_specs=P("context", "tensor"), check_vma=False
    )
```

time: 1300 us -> 427 us (0.33)
  the two profiles are of different devices: /device:TPU:17 before, /device:TPU:26 now
where the time goes in v1:
time: 427 us; the launch traced here: 425 us
  waiting for transfers between devices  146 us (34%)
  Pallas kernels  141 us (33%)
  starting transfers between devices  71 us (17%)
  blocking collectives  40.5 us (9%)
  local copies, waits for them, and re-layouts  17.4 us (4%)
  other arithmetic  8.22 us (2%)
    ppermute x35, waiting for transfers between devices, move(): return lax.ppermute(array, 'context', pairs)  133 us
    pallas_call x8, Pallas kernels, far_partial(): pl.pallas_call(functools.partial(far_body, item_count), grid_spec=pltpu.P...  76.9 us
    ppermute x35, starting transfers between devices, move(): return lax.ppermute(array, 'context', pairs)  65.3 us
    pallas_call x6, Pallas kernels, project(): pl.pallas_call(functools.partial(project_body, tuple((len(block) for bloc...  43.6 us
    all_gather x1, blocking collectives, work_table(): packed = lax.all_gather(packed, 'context', axis=0, tiled=True)  40.5 us
    pallas_call x5, Pallas kernels, merge(): pl.pallas_call(functools.partial(merge_body, len(partials), coded), grid=...  16.4 us
    ppermute x1, waiting for transfers between devices, spread_tokens(): lax.ppermute(mine, 'tensor', [(i, (i // 2 + dy) % y_size * 2 + i % 2) for...  11.2 us
  transfers between devices with their start and end apart: 40, of which 12 were waited for; matrix products, arithmetic and copies ran while one was open for 4% of the time, Pallas kernels for 30%

profile of v1, /device:TPU:26, one launch (start us, length us, event | category | flops | bytes accessed | tf_op | source)
XLA Modules:
  0.0 425.4 jit_solution(2778860691319213649)
XLA Ops:
  9.3 40.5 %all-gather = s32[8,2,33]{2,1,0:T(2,128)S(1)} all-gather(s32[1,2,33]{2,1,0:T(2,128)S(1)} %add_bitcast_fusion), channel_id=1, replica_groups=mesh['tensor'=4,'context'=8] {'context'}, dimensions={0}, use_global_device_ids=true | all-gather | bytes 2376 | tf_op jit(solution)/shard_map/all_gather | solution.py:361
  58.9 11.2 %collective-permute-done.2 = bf16[256,1280]{1,0:T(8,128)(2,1)S(1)} collective-permute-done((bf16[256,1280]{1,0:T(8,128)(2,1)}, bf16[256,1280]{1,0:T(8,128)(2,1)S(1)}, u32[]{:S(2)}, u32[]{:S(2)}) %collective-permute-start.2) | collective-permute-done | bytes 655392 | tf_op jit(solution)/shard_map/ppermute | solution.py:74
  73.9 12.4 %collective-permute-done.8.refs_9_ = bf16[256,1280]{1,0:T(8,128)(2,1)S(1)} collective-permute-done((bf16[256,1280]{1,0:T(8,128)(2,1)S(1)}, bf16[256,1280]{1,0:T(8,128)(2,1)S(1)}, u32[]{:S(2)}, u32[]{:S(2)}) %collective-permute-start.8) | collective-permute-done | bytes 655392 | tf_op jit(solution)/shard_map/ppermute | solution.py:40
  87.4 7.4 %project.7 = f32[256,1280]{1,0:T(8,128)} custom-call(bf16[256,640]{1,0:T(8,128)(2,1)} %get-tuple-element.26.refs_0_, bf16[256,640]{1,0:T(8,128)(2,1)} %get-tuple-element.25.refs_1_, bf16[256,640]{1,0:T(8,128)(2,1)} %get-tuple-element.24.refs_2_, bf16[256,640]{1,0:T(8,128)(2,1)} %get-tuple-element.23.refs_3_, bf16[640,1280]{1,0:T(8,128)(2,1)} %refs_4_.11, ...), custom_call_target="tpu_custom_call" | custom-call | flops 1677721600 | bytes 9175040 | tf_op jit(solution)/shard_map/project/pallas_call | solution.py:131
  102.7 7.2 %project.6 = f32[256,1280]{1,0:T(8,128)} custom-call(bf16[256,640]{1,0:T(8,128)(2,1)} %get-tuple-element.30.refs_0_, bf16[256,640]{1,0:T(8,128)(2,1)} %get-tuple-element.29.refs_1_, bf16[256,640]{1,0:T(8,128)(2,1)} %get-tuple-element.28.refs_2_, bf16[256,640]{1,0:T(8,128)(2,1)} %get-tuple-element.27.refs_3_, bf16[640,1280]{1,0:T(8,128)(2,1)} %refs_4_.11, ...), custom_call_target="tpu_custom_call" | custom-call | flops 1677721600 | bytes 9175040 | tf_op jit(solution)/shard_map/project/pallas_call | solution.py:131
  116.9 37.2 %collective-permute-done.10 = f32[256,1280]{1,0:T(8,128)} collective-permute-done((f32[256,1280]{1,0:T(8,128)}, f32[256,1280]{1,0:T(8,128)}, u32[]{:S(2)}, u32[]{:S(2)}) %collective-permute-start.10) | collective-permute-done | bytes 1310752 | tf_op jit(solution)/shard_map/ppermute | solution.py:40
  159.8 7.4 %collective-permute-done.27.refs_7_ = bf16[256,1280]{1,0:T(8,128)(2,1)S(1)} collective-permute-done((bf16[256,1280]{1,0:T(8,128)(2,1)S(1)}, bf16[256,1280]{1,0:T(8,128)(2,1)S(1)}, u32[]{:S(2)}, u32[]{:S(2)}) %collective-permute-start.27) | collective-permute-done | bytes 655392 | tf_op jit(solution)/shard_map/ppermute | solution.py:40
  170.3 29.9 %collective-permute-done.29.refs_9_ = bf16[256,1280]{1,0:T(8,128)(2,1)S(1)} collective-permute-done((bf16[256,1280]{1,0:T(8,128)(2,1)}, bf16[256,1280]{1,0:T(8,128)(2,1)S(1)}, u32[]{:S(2)}, u32[]{:S(2)}) %collective-permute-start.29) | collective-permute-done | bytes 655392 | tf_op jit(solution)/shard_map/ppermute | solution.py:40
  203.9 11.5 %collective-permute-done.17.q_ref = bf16[256,1280]{1,0:T(8,128)(2,1)S(1)} collective-permute-done((bf16[256,1280]{1,0:T(8,128)(2,1)}, bf16[256,1280]{1,0:T(8,128)(2,1)S(1)}, u32[]{:S(2)}, u32[]{:S(2)}) %collective-permute-start.17) | collective-permute-done | bytes 655392 | tf_op jit(solution)/shard_map/ppermute | solution.py:40
  217.3 7.1 %collective-permute-done.13.q_ref = bf16[256,1280]{1,0:T(8,128)(2,1)} collective-permute-done((bf16[256,1280]{1,0:T(8,128)(2,1)}, bf16[256,1280]{1,0:T(8,128)(2,1)}, u32[]{:S(2)}, u32[]{:S(2)}) %collective-permute-start.13) | collective-permute-done | bytes 655392 | tf_op jit(solution)/shard_map/ppermute | solution.py:40
  224.8 12.5 %far.14.refs_0_ = bf16[256,1408]{1,0:T(8,128)(2,1)} custom-call(s32[320]{0:T(512)} %reshape.547.table_ref, s32[1]{0:T(128)} %bitcast.31.source_ref, bf16[256,1280]{1,0:T(8,128)(2,1)} %collective-permute-done.21.q_ref, bf16[32,64,1280]{2,1,0:T(8,128)(2,1)} %refs_3_.15, bf16[32,64,1280]{2,1,0:T(8,128)(2,1)} %refs_3_.15, bf16[32,64,1280]{2,1,0:T(8,128)(2,1)} %refs_3_.15, ...), custom_call_target="tpu_custom_call" | custom-call | flops 2684354560 | bytes 6553600 | tf_op jit(solution)/shard_map/far/pallas_call | solution.py:240
  237.5 7.9 %far.9 = bf16[256,1408]{1,0:T(8,128)(2,1)} custom-call(s32[320]{0:T(512)} %reshape.547.table_ref, s32[1]{0:T(128)} %bitcast.26.source_ref, bf16[256,1280]{1,0:T(8,128)(2,1)} %collective-permute-done.11.q_ref, bf16[32,64,1280]{2,1,0:T(8,128)(2,1)} %refs_3_.15, bf16[32,64,1280]{2,1,0:T(8,128)(2,1)} %refs_3_.15, bf16[32,64,1280]{2,1,0:T(8,128)(2,1)} %refs_3_.15, ...), custom_call_target="tpu_custom_call" | custom-call | flops 2684354560 | bytes 6553600 | tf_op jit(solution)/shard_map/far/pallas_call | solution.py:240
  247.5 7.2 %project.9 = bf16[256,1280]{1,0:T(8,128)(2,1)} custom-call(bf16[256,640]{1,0:T(8,128)(2,1)} %get-tuple-element.26.refs_0_, bf16[256,640]{1,0:T(8,128)(2,1)} %get-tuple-element.25.refs_1_, bf16[256,640]{1,0:T(8,128)(2,1)} %get-tuple-element.24.refs_2_, bf16[256,640]{1,0:T(8,128)(2,1)} %get-tuple-element.23.refs_3_, bf16[640,1280]{1,0:T(8,128)(2,1)} %refs_4_.21, ...), custom_call_target="tpu_custom_call" | custom-call | flops 1677721600 | bytes 9175040 | tf_op jit(solution)/shard_map/project/pallas_call | solution.py:131
  254.7 7.3 %project.8 = f32[256,1280]{1,0:T(8,128)} custom-call(bf16[256,640]{1,0:T(8,128)(2,1)} %get-tuple-element.30.refs_0_, bf16[256,640]{1,0:T(8,128)(2,1)} %get-tuple-element.29.refs_1_, bf16[256,640]{1,0:T(8,128)(2,1)} %get-tuple-element.28.refs_2_, bf16[256,640]{1,0:T(8,128)(2,1)} %get-tuple-element.27.refs_3_, bf16[640,1280]{1,0:T(8,128)(2,1)} %refs_4_.21, ...), custom_call_target="tpu_custom_call" | custom-call | flops 1677721600 | bytes 9175040 | tf_op jit(solution)/shard_map/project/pallas_call | solution.py:131
  270.7 12.2 %collective-permute-start.31 = (bf16[256,1280]{1,0:T(8,128)(2,1)}, bf16[256,1280]{1,0:T(8,128)(2,1)}, u32[]{:S(2)}, u32[]{:S(2)}) collective-permute-start(bf16[256,1280]{1,0:T(8,128)(2,1)} %project.9), channel_id=1, source_target_pairs={{0,4},{1,5},{2,6},{3,7},{4,0},{5,1},{6,2},{7,3},{8,12},{9,13},{10,... | collective-permute-start | bytes 1966088 | tf_op jit(solution)/shard_map/ppermute | solution.py:40
  282.9 8.1 %far.13 = bf16[256,1408]{1,0:T(8,128)(2,1)} custom-call(s32[320]{0:T(512)} %reshape.547.table_ref, s32[1]{0:T(128)} %bitcast.30.source_ref, bf16[256,1280]{1,0:T(8,128)(2,1)} %copy-done.28, bf16[32,64,1280]{2,1,0:T(8,128)(2,1)} %refs_3_.15, bf16[32,64,1280]{2,1,0:T(8,128)(2,1)} %refs_3_.15, bf16[32,64,1280]{2,1,0:T(8,128)(2,1)} %refs_3_.15, ...), custom_call_target="tpu_custom_call" | custom-call | flops 2684354560 | bytes 6553600 | tf_op jit(solution)/shard_map/far/pallas_call | solution.py:240
  291.0 9.5 %far.11 = bf16[256,1408]{1,0:T(8,128)(2,1)} custom-call(s32[320]{0:T(512)} %reshape.547.table_ref, s32[1]{0:T(128)} %bitcast.28.source_ref, bf16[256,1280]{1,0:T(8,128)(2,1)} %collective-permute-done.14.q_ref, bf16[32,64,1280]{2,1,0:T(8,128)(2,1)} %refs_3_.15, bf16[32,64,1280]{2,1,0:T(8,128)(2,1)} %refs_3_.15, bf16[32,64,1280]{2,1,0:T(8,128)(2,1)} %refs_3_.15, ...), custom_call_target="tpu_custom_call" | custom-call | flops 2684354560 | bytes 6553600 | tf_op jit(solution)/shard_map/far/pallas_call | solution.py:240
  312.6 19.3 %collective-permute-start.38 = (bf16[256,1280]{1,0:T(8,128)(2,1)}, bf16[256,1280]{1,0:T(8,128)(2,1)S(1)}, u32[]{:S(2)}, u32[]{:S(2)}) collective-permute-start(bf16[256,1280]{1,0:T(8,128)(2,1)} %project.11), channel_id=1, source_target_pairs={{0,4},{1,5},{2,6},{3,7},{4,0},{5,1},{6,2},{7,3},{8,12},{9,13},{10,... | collective-permute-start | bytes 1966088 | tf_op jit(solution)/shard_map/ppermute | solution.py:40
  333.1 7.5 %project.10 = f32[256,1280]{1,0:T(8,128)} custom-call(bf16[256,640]{1,0:T(8,128)(2,1)} %get-tuple-element.30.refs_0_, bf16[256,640]{1,0:T(8,128)(2,1)} %get-tuple-element.29.refs_1_, bf16[256,640]{1,0:T(8,128)(2,1)} %get-tuple-element.28.refs_2_, bf16[256,640]{1,0:T(8,128)(2,1)} %get-tuple-element.27.refs_3_, bf16[640,1280]{1,0:T(8,128)(2,1)} %refs_4_.23, ...), custom_call_target="tpu_custom_call" | custom-call | flops 1677721600 | bytes 9175040 | tf_op jit(solution)/shard_map/project/pallas_call | solution.py:131
  340.6 7.3 %collective-permute-done.38 = bf16[256,1280]{1,0:T(8,128)(2,1)S(1)} collective-permute-done((bf16[256,1280]{1,0:T(8,128)(2,1)}, bf16[256,1280]{1,0:T(8,128)(2,1)S(1)}, u32[]{:S(2)}, u32[]{:S(2)}) %collective-permute-start.38) | collective-permute-done | bytes 655392 | tf_op jit(solution)/shard_map/ppermute | solution.py:40
  350.7 10.8 %far.12.refs_0_ = bf16[256,1408]{1,0:T(8,128)(2,1)} custom-call(s32[320]{0:T(512)} %reshape.547.table_ref, s32[1]{0:T(128)} %bitcast.29.source_ref, bf16[256,1280]{1,0:T(8,128)(2,1)} %copy-done.27, bf16[32,64,1280]{2,1,0:T(8,128)(2,1)} %refs_3_.15, bf16[32,64,1280]{2,1,0:T(8,128)(2,1)} %refs_3_.15, bf16[32,64,1280]{2,1,0:T(8,128)(2,1)} %refs_3_.15, ...), custom_call_target="tpu_custom_call" | custom-call | flops 2684354560 | bytes 6553600 | tf_op jit(solution)/shard_map/far/pallas_call | solution.py:240
  361.6 12.3 %far.10.refs_0_ = bf16[256,1408]{1,0:T(8,128)(2,1)} custom-call(s32[320]{0:T(512)} %reshape.547.table_ref, s32[1]{0:T(128)} %bitcast.27.source_ref, bf16[256,1280]{1,0:T(8,128)(2,1)} %collective-permute-done.13.q_ref, bf16[32,64,1280]{2,1,0:T(8,128)(2,1)} %refs_3_.15, bf16[32,64,1280]{2,1,0:T(8,128)(2,1)} %refs_3_.15, bf16[32,64,1280]{2,1,0:T(8,128)(2,1)} %refs_3_.15, ...), custom_call_target="tpu_custom_call" | custom-call | flops 2684354560 | bytes 6553600 | tf_op jit(solution)/shard_map/far/pallas_call | solution.py:240
  386.7 9.3 %far.8.refs_0_ = bf16[256,1408]{1,0:T(8,128)(2,1)} custom-call(s32[320]{0:T(512)} %reshape.547.table_ref, s32[1]{0:T(128)} %bitcast.13.source_ref, bf16[256,1280]{1,0:T(8,128)(2,1)} %add_convert_fusion.2.q_ref, bf16[32,64,1280]{2,1,0:T(8,128)(2,1)} %refs_3_.15, bf16[32,64,1280]{2,1,0:T(8,128)(2,1)} %refs_3_.15, bf16[32,64,1280]{2,1,0:T(8,128)(2,1)} %refs_3_.15, ...), custom_call_target="tpu_custom_call" | custom-call | flops 2684354560 | bytes 6553600 | tf_op jit(solution)/shard_map/far/pallas_call | solution.py:240
  404.6 14.6 %collective-permute-done.20.refs_2_ = bf16[256,1408]{1,0:T(8,128)(2,1)S(1)} collective-permute-done((bf16[256,1408]{1,0:T(8,128)(2,1)}, bf16[256,1408]{1,0:T(8,128)(2,1)S(1)}, u32[]{:S(2)}, u32[]{:S(2)}) %collective-permute-start.20) | collective-permute-done | bytes 720928 | tf_op jit(solution)/shard_map/ppermute | solution.py:40
  (209 shorter events, 107.1 us)
Async XLA Ops:
  2.3 53.7 %collective-permute-start.7 = (bf16[384,1280]{1,0:T(8,128)(2,1)}, bf16[384,1280]{1,0:T(8,128)(2,1)S(1)}, u32[]{:S(2)}, u32[]{:S(2)}) collective-permute-start(bf16[384,1280]{1,0:T(8,128)(2,1)} %slice.44), channel_id=1, source_target_pairs={{0,2},{1,3},{2,0},{3,1},{4,6},{5,7},{6,4},{7,5},{8,10},{9,11},{10,... | collective-permute-start | bytes 2949128 | tf_op jit(solution)/shard_map/ppermute | solution.py:40
  2.7 71.1 %collective-permute-start.5 = (bf16[384,1280]{1,0:T(8,128)(2,1)}, bf16[384,1280]{1,0:T(8,128)(2,1)S(1)}, u32[]{:S(2)}, u32[]{:S(2)}) collective-permute-start(bf16[384,1280]{1,0:T(8,128)(2,1)} %slice.44), channel_id=1, source_target_pairs={{0,1},{1,0},{2,3},{3,2},{4,5},{5,4},{6,7},{7,6},{8,9},{9,8},{10,11... | collective-permute-start | bytes 2949128 | tf_op jit(solution)/shard_map/ppermute | solution.py:40
  3.3 49.4 %collective-permute-start = (bf16[256,1280]{1,0:T(8,128)(2,1)}, bf16[256,1280]{1,0:T(8,128)(2,1)}, u32[]{:S(2)}, u32[]{:S(2)}) collective-permute-start(bf16[256,1280]{1,0:T(8,128)(2,1)} %param.9), channel_id=1, source_target_pairs={{0,0},{1,1},{2,2},{3,3},{4,16},{5,17},{6,18},{7,19},{8,8},{9,9},{1... | collective-permute-start | bytes 1966088 | tf_op jit(solution)/shard_map/ppermute | solution.py:68
  7.6 47.7 %collective-permute-start.4 = (bf16[256,1280]{1,0:T(8,128)(2,1)S(1)}, bf16[256,1280]{1,0:T(8,128)(2,1)S(1)}, u32[]{:S(2)}, u32[]{:S(2)}) collective-permute-start(bf16[256,1280]{1,0:T(8,128)(2,1)S(1)} %slice.43), channel_id=1, source_target_pairs={{0,1},{1,0},{2,3},{3,2},{4,5},{5,4},{6,7},{7,6},{8,9},{9,8},{10,11... | collective-permute-start | bytes 1966088 | tf_op jit(solution)/shard_map/ppermute | solution.py:40
  94.8 59.4 %collective-permute-start.10 = (f32[256,1280]{1,0:T(8,128)}, f32[256,1280]{1,0:T(8,128)}, u32[]{:S(2)}, u32[]{:S(2)}) collective-permute-start(f32[256,1280]{1,0:T(8,128)} %project.7), channel_id=1, source_target_pairs={{0,4},{1,5},{2,6},{3,7},{4,0},{5,1},{6,2},{7,3},{8,12},{9,13},{10,... | collective-permute-start | bytes 3932168 | tf_op jit(solution)/shard_map/ppermute | solution.py:40
  100.6 67.8 %collective-permute-start.28 = (bf16[384,1280]{1,0:T(8,128)(2,1)S(1)}, bf16[384,1280]{1,0:T(8,128)(2,1)S(1)}, u32[]{:S(2)}, u32[]{:S(2)}) collective-permute-start(bf16[384,1280]{1,0:T(8,128)(2,1)S(1)} %slice.46), channel_id=1, source_target_pairs={{0,2},{1,3},{2,0},{3,1},{4,6},{5,7},{6,4},{7,5},{8,10},{9,11},{10,... | collective-permute-start | bytes 2949128 | tf_op jit(solution)/shard_map/ppermute | solution.py:40
  102.4 66.0 %collective-permute-start.26 = (bf16[384,1280]{1,0:T(8,128)(2,1)S(1)}, bf16[384,1280]{1,0:T(8,128)(2,1)S(1)}, u32[]{:S(2)}, u32[]{:S(2)}) collective-permute-start(bf16[384,1280]{1,0:T(8,128)(2,1)S(1)} %slice.46), channel_id=1, source_target_pairs={{0,1},{1,0},{2,3},{3,2},{4,5},{5,4},{6,7},{7,6},{8,9},{9,8},{10,11... | collective-permute-start | bytes 2949128 | tf_op jit(solution)/shard_map/ppermute | solution.py:40
  102.4 64.8 %collective-permute-start.27 = (bf16[256,1280]{1,0:T(8,128)(2,1)S(1)}, bf16[256,1280]{1,0:T(8,128)(2,1)S(1)}, u32[]{:S(2)}, u32[]{:S(2)}) collective-permute-start(bf16[256,1280]{1,0:T(8,128)(2,1)S(1)} %slice.45), channel_id=1, source_target_pairs={{0,2},{1,3},{2,0},{3,1},{4,6},{5,7},{6,4},{7,5},{8,10},{9,11},{10,... | collective-permute-start | bytes 1966088 | tf_op jit(solution)/shard_map/ppermute | solution.py:40
  115.2 85.0 %collective-permute-start.29 = (bf16[256,1280]{1,0:T(8,128)(2,1)}, bf16[256,1280]{1,0:T(8,128)(2,1)S(1)}, u32[]{:S(2)}, u32[]{:S(2)}) collective-permute-start(bf16[256,1280]{1,0:T(8,128)(2,1)} %collective-permute-done.25.refs_5_), channel_id=1, source_target_pairs={{0,2},{1,3},{2,0},{3,1},{4,6},{5,7},{6,4},{7,5},{8,10},{9,11},{10,... | collective-permute-start | bytes 1966088 | tf_op jit(solution)/shard_map/ppermute | solution.py:40
  157.7 42.4 %collective-permute-start.32 = (bf16[256,1280]{1,0:T(8,128)(2,1)}, bf16[256,1280]{1,0:T(8,128)(2,1)S(1)}, u32[]{:S(2)}, u32[]{:S(2)}) collective-permute-start(bf16[256,1280]{1,0:T(8,128)(2,1)} %slice.47), channel_id=1, source_target_pairs={{0,1},{1,0},{2,3},{3,2},{4,5},{5,4},{6,7},{7,6},{8,9},{9,8},{10,11... | collective-permute-start | bytes 1966088 | tf_op jit(solution)/shard_map/ppermute | solution.py:40
  168.4 77.0 %collective-permute-start.30 = (bf16[384,1280]{1,0:T(8,128)(2,1)S(1)}, bf16[384,1280]{1,0:T(8,128)(2,1)}, u32[]{:S(2)}, u32[]{:S(2)}) collective-permute-start(bf16[384,1280]{1,0:T(8,128)(2,1)S(1)} %collective-permute-done.28.refs_8_), channel_id=1, source_target_pairs={{0,1},{1,0},{2,3},{3,2},{4,5},{5,4},{6,7},{7,6},{8,9},{9,8},{10,11... | collective-permute-start | bytes 2949128 | tf_op jit(solution)/shard_map/ppermute | solution.py:40
  168.4 46.9 %collective-permute-start.17 = (bf16[256,1280]{1,0:T(8,128)(2,1)}, bf16[256,1280]{1,0:T(8,128)(2,1)S(1)}, u32[]{:S(2)}, u32[]{:S(2)}) collective-permute-start(bf16[256,1280]{1,0:T(8,128)(2,1)} %add_convert_fusion.2.q_ref), channel_id=1, source_target_pairs={{0,4},{1,5},{2,6},{3,7},{4,0},{5,1},{6,2},{7,3},{8,12},{9,13},{10,... | collective-permute-start | bytes 1966088 | tf_op jit(solution)/shard_map/ppermute | solution.py:40
  200.2 47.1 %collective-permute-start.35 = (bf16[384,1280]{1,0:T(8,128)(2,1)}, bf16[384,1280]{1,0:T(8,128)(2,1)S(1)}, u32[]{:S(2)}, u32[]{:S(2)}) collective-permute-start(bf16[384,1280]{1,0:T(8,128)(2,1)} %slice.48), channel_id=1, source_target_pairs={{0,2},{1,3},{2,0},{3,1},{4,6},{5,7},{6,4},{7,5},{8,10},{9,11},{10,... | collective-permute-start | bytes 2949128 | tf_op jit(solution)/shard_map/ppermute | solution.py:40
  215.4 46.6 %collective-permute-start.22 = (bf16[256,1280]{1,0:T(8,128)(2,1)}, bf16[256,1280]{1,0:T(8,128)(2,1)S(1)}, u32[]{:S(2)}, u32[]{:S(2)}) collective-permute-start(bf16[256,1280]{1,0:T(8,128)(2,1)} %collective-permute-done.21.q_ref), channel_id=1, source_target_pairs={{0,1},{1,0},{2,3},{3,2},{4,5},{5,4},{6,7},{7,6},{8,9},{9,8},{10,11... | collective-permute-start | bytes 1966088 | tf_op jit(solution)/shard_map/ppermute | solution.py:40
  224.3 38.9 %collective-permute-start.18 = (bf16[256,1280]{1,0:T(8,128)(2,1)S(1)}, bf16[256,1280]{1,0:T(8,128)(2,1)S(1)}, u32[]{:S(2)}, u32[]{:S(2)}) collective-permute-start(bf16[256,1280]{1,0:T(8,128)(2,1)S(1)} %collective-permute-done.17.q_ref), channel_id=1, source_target_pairs={{0,1},{1,0},{2,3},{3,2},{4,5},{5,4},{6,7},{7,6},{8,9},{9,8},{10,11... | collective-permute-start | bytes 1966088 | tf_op jit(solution)/shard_map/ppermute | solution.py:40
  245.4 55.2 %collective-permute-start.33 = (bf16[384,1280]{1,0:T(8,128)(2,1)}, bf16[384,1280]{1,0:T(8,128)(2,1)S(1)}, u32[]{:S(2)}, u32[]{:S(2)}) collective-permute-start(bf16[384,1280]{1,0:T(8,128)(2,1)} %slice.48), channel_id=1, source_target_pairs={{0,1},{1,0},{2,3},{3,2},{4,5},{5,4},{6,7},{7,6},{8,9},{9,8},{10,11... | collective-permute-start | bytes 2949128 | tf_op jit(solution)/shard_map/ppermute | solution.py:40
  247.3 57.2 %collective-permute-start.37 = (bf16[384,1280]{1,0:T(8,128)(2,1)S(1)}, bf16[384,1280]{1,0:T(8,128)(2,1)S(1)}, u32[]{:S(2)}, u32[]{:S(2)}) collective-permute-start(bf16[384,1280]{1,0:T(8,128)(2,1)S(1)} %collective-permute-done.35.refs_8_), channel_id=1, source_target_pairs={{0,1},{1,0},{2,3},{3,2},{4,5},{5,4},{6,7},{7,6},{8,9},{9,8},{10,11... | collective-permute-start | bytes 2949128 | tf_op jit(solution)/shard_map/ppermute | solution.py:40
  263.2 39.3 %collective-permute-start.36 = (bf16[256,1280]{1,0:T(8,128)(2,1)S(1)}, bf16[256,1280]{1,0:T(8,128)(2,1)S(1)}, u32[]{:S(2)}, u32[]{:S(2)}) collective-permute-start(bf16[256,1280]{1,0:T(8,128)(2,1)S(1)} %collective-permute-done.32.refs_5_), channel_id=1, source_target_pairs={{0,2},{1,3},{2,0},{3,1},{4,6},{5,7},{6,4},{7,5},{8,10},{9,11},{10,... | collective-permute-start | bytes 1966088 | tf_op jit(solution)/shard_map/ppermute | solution.py:40
  270.7 41.8 %collective-permute-start.31 = (bf16[256,1280]{1,0:T(8,128)(2,1)}, bf16[256,1280]{1,0:T(8,128)(2,1)}, u32[]{:S(2)}, u32[]{:S(2)}) collective-permute-start(bf16[256,1280]{1,0:T(8,128)(2,1)} %project.9), channel_id=1, source_target_pairs={{0,4},{1,5},{2,6},{3,7},{4,0},{5,1},{6,2},{7,3},{8,12},{9,13},{10,... | collective-permute-start | bytes 1966088 | tf_op jit(solution)/shard_map/ppermute | solution.py:40
  300.5 95.5 %collective-permute-start.12 = (bf16[256,1408]{1,0:T(8,128)(2,1)}, bf16[256,1408]{1,0:T(8,128)(2,1)S(1)}, u32[]{:S(2)}, u32[]{:S(2)}) collective-permute-start(bf16[256,1408]{1,0:T(8,128)(2,1)} %far.9), channel_id=1, source_target_pairs={{0,1},{1,0},{2,3},{3,2},{4,5},{5,4},{6,7},{7,6},{8,9},{9,8},{10,11... | collective-permute-start | bytes 2162696 | tf_op jit(solution)/shard_map/ppermute | solution.py:40
  300.6 73.4 %collective-permute-start.23 = (bf16[256,1408]{1,0:T(8,128)(2,1)}, bf16[256,1408]{1,0:T(8,128)(2,1)}, u32[]{:S(2)}, u32[]{:S(2)}) collective-permute-start(bf16[256,1408]{1,0:T(8,128)(2,1)} %far.15), channel_id=1, source_target_pairs={{0,1},{1,0},{2,3},{3,2},{4,5},{5,4},{6,7},{7,6},{8,9},{9,8},{10,11... | collective-permute-start | bytes 2162696 | tf_op jit(solution)/shard_map/ppermute | solution.py:40
  302.6 74.4 %collective-permute-start.19 = (bf16[256,1408]{1,0:T(8,128)(2,1)}, bf16[256,1408]{1,0:T(8,128)(2,1)S(1)}, u32[]{:S(2)}, u32[]{:S(2)}) collective-permute-start(bf16[256,1408]{1,0:T(8,128)(2,1)} %far.13), channel_id=1, source_target_pairs={{0,1},{1,0},{2,3},{3,2},{4,5},{5,4},{6,7},{7,6},{8,9},{9,8},{10,11... | collective-permute-start | bytes 2162696 | tf_op jit(solution)/shard_map/ppermute | solution.py:40
  304.5 76.3 %collective-permute-start.15 = (bf16[256,1408]{1,0:T(8,128)(2,1)}, bf16[256,1408]{1,0:T(8,128)(2,1)S(1)}, u32[]{:S(2)}, u32[]{:S(2)}) collective-permute-start(bf16[256,1408]{1,0:T(8,128)(2,1)} %far.11), channel_id=1, source_target_pairs={{0,1},{1,0},{2,3},{3,2},{4,5},{5,4},{6,7},{7,6},{8,9},{9,8},{10,11... | collective-permute-start | bytes 2162696 | tf_op jit(solution)/shard_map/ppermute | solution.py:40
  349.4 50.4 %collective-permute-start.39 = (bf16[2,128,1280]{2,1,0:T(8,128)(2,1)S(1)}, bf16[2,128,1280]{2,1,0:T(8,128)(2,1)S(1)}, u32[]{:S(2)}, u32[]{:S(2)}) collective-permute-start(bf16[2,128,1280]{2,1,0:T(8,128)(2,1)S(1)} %pad_maximum_fusion), channel_id=1, source_target_pairs={{0,1},{1,2},{2,3},{3,4},{4,5},{5,6},{6,7},{8,9},{9,10},{10,11},{11... | collective-permute-start | bytes 1966088 | tf_op jit(solution)/shard_map/ppermute | solution.py:463
  (49 other events, 928.3 us)
